TPU v7x, 256 devices: a whole 4x4x8 slice. The times are simulated.
256 devices in a mesh: bank: 16 (over z, core), zero: 16 (over y, x).
Axes of the slice: x: 4, y: 4, z: 8, core: 2. Of those that a mesh axis runs over, the one named last changes fastest.
Arguments:
- master_down: float32 [64, 1024, 2048], P('bank', None, 'zero'), may hold values from -0.25 to 0.25
- second_down: bfloat16 [64, 1024, 2048], P('bank', None, 'zero'), may hold values from -0.09375 to 0.09375
- router_weight: float32 [2048, 64], P('zero', 'bank'), may hold values from -0.125 to 0.125
- router_gain: float32 [2048], P('zero'), may hold values from 0.25 to 1.75
Outputs:
- final_down: bfloat16 [64, 1024, 2048], P('bank')
- scale_down: float32 [64, 1024], P('bank')
- serve_router: bfloat16 [2048, 64], replicated
All inputs are finite; a program needn't handle non-finite values. Where the computation divides by a largest or mean magnitude, that divisor is 1e-20 or more.
Results may differ from a plain program's by a relative error of at most 0.001.
Values may be sent and summed in bfloat16 or wider, within the bound.
A program may use at most 128 MiB of HBM per device.

v0:
```python
import jax
import jax.numpy as jnp
from jax import lax
from jax.sharding import PartitionSpec as P


def from_everyone(value, axis):
    count = lax.axis_size(axis)
    return lax.all_to_all(
        jnp.broadcast_to(value[None], (count, *value.shape)), axis, 0, 0, tiled=True
    )


def over_copies(value, axis):
    everything = from_everyone(value, axis)
    return jnp.max(everything, axis=0)


def joined_along(pieces, dim):
    pieces = jnp.moveaxis(pieces, 0, dim)
    dims = pieces.shape
    return pieces.reshape(*dims[:dim], dims[dim] * dims[dim + 1], *dims[dim + 2 :])


def collect(value, axis, dim):
    return joined_along(from_everyone(value, axis), dim)


def shards(master_down, second_down, router_weight, router_gain):
    merged_down = master_down + second_down.astype(jnp.float32)
    scale_down = over_copies(jnp.max(jnp.abs(merged_down), axis=2), "zero")
    narrow_down = (merged_down / jnp.expand_dims(scale_down, 2)).astype(jnp.bfloat16)
    final_down = lax.all_gather(narrow_down, "zero", axis=2, tiled=True)
    part_router = (router_weight * router_gain[:, None]).astype(jnp.bfloat16)
    row_router = collect(part_router, "zero", 0)
    serve_router = lax.all_gather(row_router, "bank", axis=1, tiled=True)
    return (final_down, scale_down, serve_router)


def solution(mesh):
    return jax.shard_map(
        shards,
        mesh=mesh,
        in_specs=(P("bank", None, "zero"), P("bank", None, "zero"), P("zero", "bank"), P("zero")),
        out_specs=(P("bank", None, None), P("bank", None), P()),
        check_vma=False,
    )
```

profile of v0, /device:TPU:2, one launch (start us, length us, event | category | flops | bytes accessed | tf_op | source)
XLA Modules:
  0.0 171.8 jit_solution(3253551120182133146)
XLA Ops:
  7.2 0.0 copy-start
  7.2 0.0 copy-start.1
  7.2 0.0 all-gather.3.cloned.1.call-start
  7.2 2.6 %abs_reduce_fusion = f32[4,1024]{1,0:T(4,128)S(1)} fusion(f32[4,1024,128]{2,1,0:T(8,128)} %param.4, bf16[4,1024,128]{2,1,0:T(8,128)(2,1)} %param.5), kind=kLoop, calls=%fused_computation.1 | loop fusion | flops 2093056 | bytes 3162112 | tf_op jit(solution)/shard_map/reduce_max | solution.py:31
  9.9 14.6 %all_to_all.10 = f32[16,4,1024]{2,1,0:T(4,128)S(1)} all-to-all(f32[16,4,1024]{2,1,0:T(4,128)S(1)} %broadcast_in_dim.4), channel_id=1, replica_groups=mesh['bank'=16,'zero'=16] {'zero'}, dimensions={0} | all-to-all | bytes 524288 | tf_op jit(solution)/shard_map/all_to_all | solution.py:9
  24.5 0.1 reduce_max.19
  24.6 0.0 copy-done
  24.6 0.0 copy-done.1
  24.6 0.0 copy-start.2
  24.6 0.0 copy-start.3
  24.6 0.0 copy-start.4
  24.6 1.5 divide_convert_fusion
  26.1 0.0 copy-done.2
  26.1 0.0 all-gather.3.cloned.1.call-update
  26.2 0.0 copy-done.3
  26.2 0.0 copy-done.4
  26.2 10.5 %all_to_all.11 = bf16[16,128,4]{1,2,0:T(4,128)(2,1)S(1)} all-to-all(bf16[16,128,4]{1,2,0:T(4,128)(2,1)S(1)} %broadcast_in_dim.5), channel_id=1, replica_groups=mesh['bank'=16,'zero'=16] {'zero'}, dimensions={0} | all-to-all | bytes 32768 | tf_op jit(solution)/shard_map/all_to_all | solution.py:9
  36.7 20.7 %all-gather = bf16[16,4,2048]{2,1,0:T(4,128)(2,1)S(1)} all-gather(bf16[1,4,2048]{2,1,0:T(4,128)(2,1)S(1)} %bitcast.7), channel_id=1, replica_groups=mesh['bank'=16,'zero'=16] {'bank'}, dimensions={0}, use_global_device_ids=true | all-gather | bytes 278528 | tf_op jit(solution)/shard_map/all_gather | solution.py:36
  57.4 0.8 reshape.15
  58.1 92.7 %all-gather.3.cloned.1.call-done = bf16[4,1024,2048]{2,1,0:T(8,128)(2,1)} async-done(((bf16[4,1024,128]{2,1,0:T(8,128)(2,1)}), bf16[4,1024,2048]{2,1,0:T(8,128)(2,1)}) %all-gather.3.cloned.1.call-update) | async-done | bytes 16777232 | tf_op jit(solution)/shard_map/all_gather | solution.py:33
  150.8 14.2 %copy.10 = bf16[4,1024,2048]{2,1,0:T(8,128)(2,1)} copy(bf16[4,1024,2048]{2,1,0:T(8,128)(2,1)} %all-gather.3.cloned.1.call-done) | data formatting | bytes 33554432
  (3 shorter events, 0.1 us)
Async XLA Ops:
  7.2 17.4 %copy-start = (f32[4,1024,128]{2,1,0:T(8,128)S(1)}, f32[4,1024,128]{2,1,0:T(8,128)}, u32[]{:S(2)}) copy-start(f32[4,1024,128]{2,1,0:T(8,128)} %param.4) | copy-start | bytes 6291460
  7.2 17.4 %copy-start.1 = (bf16[4,1024,128]{2,1,0:T(8,128)(2,1)S(1)}, bf16[4,1024,128]{2,1,0:T(8,128)(2,1)}, u32[]{:S(2)}) copy-start(bf16[4,1024,128]{2,1,0:T(8,128)(2,1)} %param.5) | copy-start | bytes 3145732
  7.2 143.6 %all-gather.3.cloned.1.call-start = ((), (), s32[]{:S(2)}) async-start(), calls=%async_computation.2 | async-start | bytes 17825792 | tf_op jit(solution)/shard_map/all_gather | solution.py:33
  24.6 1.6 copy-start.2
  24.6 1.6 copy-start.3
  24.6 1.6 copy-start.4
Sparse Core Ops, SparseCore 0:
  26.3 124.4 all-gather.2
where the time goes:
time: 172 us
  waiting for transfers between devices  92.7 us (54%)
  blocking collectives  45.8 us (27%)
  local copies, waits for them, and re-layouts  15 us (9%)
  between operations  14.1 us (8%)
  other arithmetic  4.21 us (2%)
    all_gather x1, waiting for transfers between devices, shards(): final_down = lax.all_gather(narrow_down, 'zero', axis=2, tiled=True)  92.7 us
    all_to_all x2, blocking collectives, from_everyone(): lax.all_to_all(jnp.broadcast_to(value[None], (count, *value.shape)), axis...  25.1 us
    all_gather x1, blocking collectives, shards(): serve_router = lax.all_gather(row_router, 'bank', axis=1, tiled=True)  20.7 us
    unnamed x12, local copies, waits for them, and re-layouts  14.9 us
  transfers between devices with their start and end apart: 1, of which 1 were waited for; matrix products, arithmetic and copies ran while one was open for 0% of the time, Pallas kernels for 0%

commit v1 on v0

--- a/solution.py
+++ b/solution.py
@@ -2,6 +2,12 @@
 import jax.numpy as jnp
 from jax import lax
 from jax.sharding import PartitionSpec as P
+
+
+def gather_blocks(array, axis, dim):
+    parts = lax.all_gather(array, axis, axis=0, tiled=False)
+    whole = jnp.concatenate(parts, axis=dim)
+    return whole
 
 
 def from_everyone(value, axis):
@@ -30,7 +36,7 @@
     merged_down = master_down + second_down.astype(jnp.float32)
     scale_down = over_copies(jnp.max(jnp.abs(merged_down), axis=2), "zero")
     narrow_down = (merged_down / jnp.expand_dims(scale_down, 2)).astype(jnp.bfloat16)
-    final_down = lax.all_gather(narrow_down, "zero", axis=2, tiled=True)
+    final_down = gather_blocks(narrow_down, "zero", 2)
     part_router = (router_weight * router_gain[:, None]).astype(jnp.bfloat16)
     row_router = collect(part_router, "zero", 0)
     serve_router = lax.all_gather(row_router, "bank", axis=1, tiled=True)

time: 172 us -> 166 us (0.965)
  waiting for transfers between devices: 92.7 us -> 84.4 us
    reshape x0 -> x1, local copies, waits for them, and re-layouts: none -> 15.3 us  [gather_blocks(): whole = jnp.concatenate(parts, axis=dim)]
    unnamed x12 -> x11, local copies, waits for them, and re-layouts: 14.9 us -> 0.79 us
    all_gather x1, waiting for transfers between devices: 92.7 us -> 84.3 us  [gather_blocks(): parts = lax.all_gather(array, axis, axis=0, tiled=False)]
where the time goes in v1:
time: 166 us; the launch traced here: 165 us
  waiting for transfers between devices  84.4 us (51%)
  blocking collectives  45.8 us (28%)
  local copies, waits for them, and re-layouts  16.2 us (10%)
  between operations  14.1 us (8%)
  other arithmetic  4.21 us (3%)
    all_gather x1, waiting for transfers between devices, gather_blocks(): parts = lax.all_gather(array, axis, axis=0, tiled=False)  84.3 us
    all_to_all x2, blocking collectives, from_everyone(): lax.all_to_all(jnp.broadcast_to(value[None], (count, *value.shape)), axis...  25.1 us
    all_gather x1, blocking collectives, shards(): serve_router = lax.all_gather(row_router, 'bank', axis=1, tiled=True)  20.7 us
    reshape x1, local copies, waits for them, and re-layouts, gather_blocks(): whole = jnp.concatenate(parts, axis=dim)  15.3 us
  transfers between devices with their start and end apart: 1, of which 1 were waited for; matrix products, arithmetic and copies ran while one was open for 0% of the time, Pallas kernels for 0%

profile of v1, /device:TPU:2, one launch (start us, length us, event | category | flops | bytes accessed | tf_op | source)
XLA Modules:
  0.0 164.7 jit_solution(3314378420289406427)
XLA Ops:
  7.2 0.0 copy-start
  7.2 0.0 copy-start.1
  7.2 0.0 all-gather.4.cloned.1.call-start
  7.2 2.6 %abs_reduce_fusion = f32[4,1024]{1,0:T(4,128)S(1)} fusion(f32[4,1024,128]{2,1,0:T(8,128)} %param.4, bf16[4,1024,128]{2,1,0:T(8,128)(2,1)} %param.5), kind=kLoop, calls=%fused_computation.2 | loop fusion | flops 2093056 | bytes 3162112 | tf_op jit(solution)/shard_map/reduce_max | solution.py:37
  9.9 14.6 %all_to_all.10 = f32[16,4,1024]{2,1,0:T(4,128)S(1)} all-to-all(f32[16,4,1024]{2,1,0:T(4,128)S(1)} %broadcast_in_dim.4), channel_id=1, replica_groups=mesh['bank'=16,'zero'=16] {'zero'}, dimensions={0} | all-to-all | bytes 524288 | tf_op jit(solution)/shard_map/all_to_all | solution.py:15
  24.5 0.1 reduce_max.19
  24.6 0.0 copy-done
  24.6 0.0 copy-done.1
  24.6 0.0 copy-start.2
  24.6 0.0 copy-start.3
  24.6 0.0 copy-start.4
  24.6 1.5 divide_convert_fusion
  26.1 0.0 copy-done.2
  26.1 0.0 all-gather.4.cloned.1.call-update
  26.2 0.0 copy-done.3
  26.2 0.0 copy-done.4
  26.2 10.5 %all_to_all.11 = bf16[16,128,4]{1,2,0:T(4,128)(2,1)S(1)} all-to-all(bf16[16,128,4]{1,2,0:T(4,128)(2,1)S(1)} %broadcast_in_dim.5), channel_id=1, replica_groups=mesh['bank'=16,'zero'=16] {'zero'}, dimensions={0} | all-to-all | bytes 32768 | tf_op jit(solution)/shard_map/all_to_all | solution.py:15
  36.7 20.7 %all-gather.1 = bf16[16,4,2048]{2,1,0:T(4,128)(2,1)S(1)} all-gather(bf16[1,4,2048]{2,1,0:T(4,128)(2,1)S(1)} %bitcast.16), channel_id=1, replica_groups=mesh['bank'=16,'zero'=16] {'bank'}, dimensions={0}, use_global_device_ids=true | all-gather | bytes 278528 | tf_op jit(solution)/shard_map/all_gather | solution.py:42
  57.4 0.8 reshape.24
  58.1 84.3 %all-gather.4.cloned.1.call-done = bf16[64,1024,128]{2,1,0:T(8,128)(2,1)} async-done(((bf16[4,1024,128]{2,1,0:T(8,128)(2,1)}), bf16[64,1024,128]{2,1,0:T(8,128)(2,1)}) %all-gather.4.cloned.1.call-update) | async-done | bytes 16777232 | tf_op jit(solution)/shard_map/all_gather | solution.py:8
  142.5 15.3 %copy.15 = bf16[16,4,128,8,128]{4,3,0,2,1:T(8,128)(2,1)} copy(bf16[16,4,128,8,128]{4,3,2,1,0:T(8,128)(2,1)} %bitcast.13) | data formatting | bytes 33554432 | tf_op jit(solution)/shard_map/reshape | solution.py:9
  (3 shorter events, 0.1 us)
Async XLA Ops:
  7.2 17.4 %copy-start = (f32[4,1024,128]{2,1,0:T(8,128)S(1)}, f32[4,1024,128]{2,1,0:T(8,128)}, u32[]{:S(2)}) copy-start(f32[4,1024,128]{2,1,0:T(8,128)} %param.4) | copy-start | bytes 6291460
  7.2 17.4 %copy-start.1 = (bf16[4,1024,128]{2,1,0:T(8,128)(2,1)S(1)}, bf16[4,1024,128]{2,1,0:T(8,128)(2,1)}, u32[]{:S(2)}) copy-start(bf16[4,1024,128]{2,1,0:T(8,128)(2,1)} %param.5) | copy-start | bytes 3145732
  7.2 135.3 %all-gather.4.cloned.1.call-start = ((), (), s32[]{:S(2)}) async-start(), calls=%async_computation.2 | async-start | bytes 17825792 | tf_op jit(solution)/shard_map/all_gather | solution.py:8
  24.6 1.6 copy-start.2
  24.6 1.6 copy-start.3
  24.6 1.6 copy-start.4
Sparse Core Ops, SparseCore 0:
  26.3 116.1 all-gather.3
